TPU v7x, 1024 devices: a whole 4x4x32 slice. The times are simulated.
1024 devices in a mesh: lat: 16 (over x_lo, y, core), lon: 64 (over z, x_hi).
Axes of the slice: x: 4 (x_hi: 2, x_lo: 2; x = x_hi * 2 + x_lo), y: 4, z: 32, core: 2. Of those that a mesh axis runs over, the one named last changes fastest.
Arguments:
- tracers: bfloat16 [10, 4, 256, 8192], P(None, None, 'lat', 'lon'), may hold values from -6 to 6
- winds: float32 [3, 4, 256, 8192], P(None, None, 'lat', 'lon'), may hold values from -2.5 to 2.5
- zonal_shift: int32 [256], P('lat'), may hold values from 0 to 8191
Outputs:
- new_tracers: bfloat16 [10, 4, 256, 8192], P(None, None, 'lat', 'lon')
- displacement: float32 [3, 4, 256, 8192], P(None, None, 'lat', 'lon')
All inputs are finite; a program needn't handle non-finite values.
Results may differ from a plain program's by a relative error of at most 0.001.
Values may be sent and summed in bfloat16 or wider, within the bound.
No kernel may reach another device: no remote copies, remote signals or barrier semaphores. Data moves between devices by JAX's collectives and lax.ppermute only.
A program may use at most 64 MiB of HBM per device.

v0:
```python
import jax
import jax.numpy as jnp
from jax import lax
from jax.sharding import PartitionSpec as P

ITERS = 3
RIM = 4


def shifted_2(x, axis, by):
    length = lax.axis_size(axis)
    return lax.ppermute(x, axis, [(i, (i + by) % length) for i in range(length)])


def padded(block, sides, width):
    for axis, dim in sides:
        count = lax.axis_size(axis)
        forward = [(i, i + 1) for i in range(count - 1)]
        forward.append((count - 1, 0))
        backward = [(target, source) for source, target in forward]
        low = lax.ppermute(
            lax.slice_in_dim(block, block.shape[dim] - width, None, axis=dim), axis, forward
        )
        high = lax.ppermute(lax.slice_in_dim(block, 0, width, axis=dim), axis, backward)
        block = jnp.concatenate([low, block, high], axis=dim)
    return block


def cubic_weights(frac):
    return (
        -frac * (frac - 1.0) * (frac - 2.0) / 6.0,
        (frac + 1.0) * (frac - 1.0) * (frac - 2.0) / 2.0,
        -(frac + 1.0) * frac * (frac - 2.0) / 2.0,
        (frac + 1.0) * frac * (frac - 1.0) / 6.0,
    )


def spread(base, weights, lowest, highest):
    listed = []
    for target in range(lowest, highest + 1):
        summed = jnp.zeros(base.shape, jnp.float32)
        for a in range(len(weights)):
            summed = summed + jnp.where(base + a == target, weights[a], 0.0)
        listed.append(summed)
    return listed


def pole_zero(block, width, anchor, total_rows):
    rowpos = lax.broadcasted_iota(jnp.int32, (block.shape[2], 1), 0) + anchor - width
    keep = (rowpos >= 0) & (rowpos < total_rows)
    return jnp.where(keep, block, jnp.zeros_like(block))


def translate_doubling(block, shifts):
    cols = block.shape[3]
    sectors = shifts // cols
    within = shifts - sectors * cols
    steps = (lax.axis_size("lon") - 1).bit_length()
    for bit in range(steps):
        moved = shifted_2(block, "lon", 1 << bit)
        chosen = (sectors >> bit & 1 == 1)[:, None]
        block = jnp.where(chosen, moved, block)
    western = shifted_2(block, "lon", 1)
    joined = jnp.concatenate([western, block], axis=3)
    offset = cols - within
    for bit in range(cols.bit_length()):
        step_cols = 1 << bit
        padding = jnp.zeros(joined.shape[:3] + (step_cols,), joined.dtype)
        shifted = jnp.concatenate([joined[:, :, :, step_cols:], padding], axis=3)
        chosen = (offset >> bit & 1 == 1)[:, None]
        joined = jnp.where(chosen, shifted, joined)
    return joined[:, :, :, :cols]


def local(tracers, winds, zonal_shift):
    ntrac, levels, rows, cols = tracers.shape
    total_rows = rows * lax.axis_size("lat")
    anchor = lax.axis_index("lat") * rows
    shape = (levels, rows, cols)
    kpos = lax.broadcasted_iota(jnp.float32, shape, 0)
    kint = lax.broadcasted_iota(jnp.int32, shape, 0)
    growi = lax.broadcasted_iota(jnp.int32, shape, 1) + anchor
    gpos = growi.astype(jnp.float32)
    wide = padded(winds, (("lat", 2), ("lon", 3)), 2)
    wide = pole_zero(wide, 2, anchor, total_rows)
    wide = jnp.pad(wide, ((0, 0), (2, 2), (0, 0), (0, 0)))
    disp = winds
    for step in range(ITERS):
        zlev = jnp.clip(kpos - 0.5 * disp[0], 0.0, levels - 1.0)
        ylat = jnp.clip(gpos - 0.5 * disp[1], 0.0, total_rows - 1.0)
        wind_xrel = -0.5 * disp[2]
        wind_zb = jnp.floor(zlev)
        wind_yb = jnp.floor(ylat)
        wind_xb = jnp.floor(wind_xrel)
        tz = zlev - wind_zb
        ty = ylat - wind_yb
        tx = wind_xrel - wind_xb
        wind_z_weights = spread(wind_zb.astype(jnp.int32) - kint, (1.0 - tz, tz), -2, 2)
        wind_y_weights = spread(wind_yb.astype(jnp.int32) - growi, (1.0 - ty, ty), -2, 2)
        wind_x_weights = spread(wind_xb.astype(jnp.int32), (1.0 - tx, tx), -2, 2)
        total = jnp.zeros((3,) + shape, jnp.float32)
        for wind_iz in range(5):
            wind_plane = jnp.zeros((3,) + shape, jnp.float32)
            for wind_iy in range(5):
                wind_line = jnp.zeros((3,) + shape, jnp.float32)
                for wind_ix in range(5):
                    wind_line = (
                        wind_line
                        + wind_x_weights[wind_ix]
                        * wide[
                            :,
                            wind_iz : wind_iz + levels,
                            wind_iy : wind_iy + rows,
                            wind_ix : wind_ix + cols,
                        ]
                    )
                wind_plane = wind_plane + wind_y_weights[wind_iy] * wind_line
            total = total + wind_z_weights[wind_iz] * wind_plane
        disp = total
    moved = translate_doubling(tracers, zonal_shift)
    source = padded(moved, (("lat", 2), ("lon", 3)), RIM)
    source = pole_zero(source, RIM, anchor, total_rows)
    source = jnp.pad(source, ((0, 0), (4, 4), (0, 0), (0, 0)))
    lanes = []
    for oy in range(-4, 5):
        lanes.append(source[:, :, RIM + oy : RIM + oy + rows, RIM - 4 : RIM + cols + 4])
    zdep = jnp.clip(kpos - disp[0], 0.0, levels - 1.0)
    ydep = jnp.clip(gpos - disp[1], 0.0, total_rows - 1.0)
    xrel = -disp[2]
    zb = jnp.floor(zdep)
    yb = jnp.floor(ydep)
    xb = jnp.floor(xrel)
    z_weights = spread(zb.astype(jnp.int32) - kint - 1, cubic_weights(zdep - zb), -4, 4)
    y_weights = spread(yb.astype(jnp.int32) - growi - 1, cubic_weights(ydep - yb), -4, 4)
    x_weights = spread(xb.astype(jnp.int32) - 1, cubic_weights(xrel - xb), -4, 4)
    result = jnp.zeros((ntrac,) + shape, jnp.float32)
    for iz in range(9):
        plane = jnp.zeros((ntrac,) + shape, jnp.float32)
        for iy in range(9):
            line = jnp.zeros((ntrac,) + shape, jnp.float32)
            for ix in range(9):
                line = line + x_weights[ix] * lanes[iy][:, iz : iz + levels, :, ix : ix + cols]
            plane = plane + y_weights[iy] * line
        result = result + z_weights[iz] * plane
    return (result.astype(jnp.bfloat16), disp)


def solution(mesh):
    return jax.shard_map(
        local,
        mesh=mesh,
        in_specs=(P(None, None, "lat", "lon"), P(None, None, "lat", "lon"), P("lat")),
        out_specs=(P(None, None, "lat", "lon"), P(None, None, "lat", "lon")),
        check_vma=False,
    )
```

profile of v0, /device:TPU:25, one launch (start us, length us, event | category | flops | bytes accessed | tf_op | source)
XLA Modules:
  0.0 242.2 jit_solution(14677086848175550095)
XLA Ops:
  0.6 0.9 fusion.45
  1.5 3.3 %collective-permute-start = (f32[3,4,2,128]{3,2,1,0:T(2,128)S(1)}, f32[3,4,2,128]{3,2,1,0:T(2,128)S(1)}, u32[]{:S(2)}, u32[]{:S(2)}) collective-permute-start(f32[3,4,2,128]{3,2,1,0:T(2,128)S(1)} %get-tuple-element.98), channel_id=1, source_target_pairs={{0,64},{64,128},{128,192},{192,256},{256,320},{320,384},{384,448},... | collective-permute-start | bytes 36872 | tf_op jit(solution)/shard_map/ppermute | solution.py:21
  4.9 1.9 collective-permute-start.1
  6.8 4.4 %collective-permute-start.4 = (bf16[10,4,16,128]{3,2,1,0:T(8,128)(2,1)}, bf16[10,4,16,128]{3,2,1,0:T(8,128)(2,1)S(1)}, u32[]{:S(2)}, u32[]{:S(2)}) collective-permute-start(bf16[10,4,16,128]{3,2,1,0:T(8,128)(2,1)} %param.3), channel_id=1, source_target_pairs={{0,1},{1,2},{2,3},{3,4},{4,5},{5,6},{6,7},{7,8},{8,9},{9,10},{10,1... | collective-permute-start | bytes 491528 | tf_op jit(solution)/shard_map/ppermute | solution.py:12
  11.2 0.7 and_compare_fusion.13
  11.9 0.9 add_bitcast_fusion.69
  13.0 3.9 %collective-permute-start.2 = (f32[3,4,20,2]{3,2,1,0:T(8,128)S(1)}, f32[3,4,20,2]{3,2,1,0:T(8,128)S(1)}, u32[]{:S(2)}, u32[]{:S(2)}) collective-permute-start(f32[3,4,20,2]{3,2,1,0:T(8,128)S(1)} %get-tuple-element.20), channel_id=1, source_target_pairs={{0,1},{1,2},{2,3},{3,4},{4,5},{5,6},{6,7},{7,8},{8,9},{9,10},{10,1... | collective-permute-start | bytes 5768 | tf_op jit(solution)/shard_map/ppermute | solution.py:21
  16.9 17.8 %collective-permute-start.3 = (f32[3,4,20,2]{3,2,1,0:T(8,128)S(1)}, f32[3,4,20,2]{3,2,1,0:T(8,128)S(1)}, u32[]{:S(2)}, u32[]{:S(2)}) collective-permute-start(f32[3,4,20,2]{3,2,1,0:T(8,128)S(1)} %get-tuple-element.21), channel_id=1, source_target_pairs={{1,0},{2,1},{3,2},{4,3},{5,4},{6,5},{7,6},{8,7},{9,8},{10,9},{11,1... | collective-permute-start | bytes 5768 | tf_op jit(solution)/shard_map/ppermute | solution.py:24
  34.8 2.2 collective-permute-done.2
  37.0 1.3 collective-permute-done.3
  38.2 0.2 maximum_select_fusion.1
  38.6 1.9 collective-permute-start.5
  40.5 1.8 multiply_add_fusion.6
  42.4 7.4 %collective-permute-done.5 = bf16[10,4,16,128]{3,2,1,0:T(8,128)(2,1)S(1)} collective-permute-done((bf16[10,4,16,128]{3,2,1,0:T(8,128)(2,1)S(1)}, bf16[10,4,16,128]{3,2,1,0:T(8,128)(2,1)S(1)}, u32[]{:S(2)}, u32[]{:S(2)}) %collective-permute-start.5) | collective-permute-done | bytes 163872 | tf_op jit(solution)/shard_map/ppermute | solution.py:12
  49.8 1.9 collective-permute-start.6
  51.9 10.3 %collective-permute-done.6 = bf16[10,4,16,128]{3,2,1,0:T(8,128)(2,1)S(1)} collective-permute-done((bf16[10,4,16,128]{3,2,1,0:T(8,128)(2,1)S(1)}, bf16[10,4,16,128]{3,2,1,0:T(8,128)(2,1)S(1)}, u32[]{:S(2)}, u32[]{:S(2)}) %collective-permute-start.6) | collective-permute-done | bytes 163872 | tf_op jit(solution)/shard_map/ppermute | solution.py:12
  62.3 1.9 collective-permute-start.7
  64.2 1.8 multiply_add_fusion.5
  66.1 16.5 %collective-permute-done.7 = bf16[10,4,16,128]{3,2,1,0:T(8,128)(2,1)S(1)} collective-permute-done((bf16[10,4,16,128]{3,2,1,0:T(8,128)(2,1)S(1)}, bf16[10,4,16,128]{3,2,1,0:T(8,128)(2,1)S(1)}, u32[]{:S(2)}, u32[]{:S(2)}) %collective-permute-start.7) | collective-permute-done | bytes 163872 | tf_op jit(solution)/shard_map/ppermute | solution.py:12
  82.6 1.9 collective-permute-start.8
  84.7 30.9 %collective-permute-done.8 = bf16[10,4,16,128]{3,2,1,0:T(8,128)(2,1)S(1)} collective-permute-done((bf16[10,4,16,128]{3,2,1,0:T(8,128)(2,1)S(1)}, bf16[10,4,16,128]{3,2,1,0:T(8,128)(2,1)S(1)}, u32[]{:S(2)}, u32[]{:S(2)}) %collective-permute-start.8) | collective-permute-done | bytes 163872 | tf_op jit(solution)/shard_map/ppermute | solution.py:12
  115.7 13.8 %collective-permute-start.9 = (bf16[10,4,16,128]{3,2,1,0:T(8,128)(2,1)S(1)}, bf16[10,4,16,128]{3,2,1,0:T(8,128)(2,1)S(1)}, u32[]{:S(2)}, u32[]{:S(2)}) collective-permute-start(bf16[10,4,16,128]{3,2,1,0:T(8,128)(2,1)S(1)} %broadcast_select_fusion.4), channel_id=1, source_target_pairs={{0,32},{1,33},{2,34},{3,35},{4,36},{5,37},{6,38},{7,39},{8,40},{9,... | collective-permute-start | bytes 491528 | tf_op jit(solution)/shard_map/ppermute | solution.py:12
  129.6 1.8 multiply_add_fusion.4
  131.4 24.9 %collective-permute-done.9 = bf16[10,4,16,128]{3,2,1,0:T(8,128)(2,1)S(1)} collective-permute-done((bf16[10,4,16,128]{3,2,1,0:T(8,128)(2,1)S(1)}, bf16[10,4,16,128]{3,2,1,0:T(8,128)(2,1)S(1)}, u32[]{:S(2)}, u32[]{:S(2)}) %collective-permute-start.9) | collective-permute-done | bytes 163872 | tf_op jit(solution)/shard_map/ppermute | solution.py:12
  156.5 1.9 collective-permute-start.10
  158.4 0.3 add_bitcast_fusion.2
  158.6 8.5 %collective-permute-done.10 = bf16[10,4,16,128]{3,2,1,0:T(8,128)(2,1)S(1)} collective-permute-done((bf16[10,4,16,128]{3,2,1,0:T(8,128)(2,1)S(1)}, bf16[10,4,16,128]{3,2,1,0:T(8,128)(2,1)S(1)}, u32[]{:S(2)}, u32[]{:S(2)}) %collective-permute-start.10) | collective-permute-done | bytes 163872 | tf_op jit(solution)/shard_map/ppermute | solution.py:12
  167.1 0.2 fusion
  167.3 0.2 fusion.1
  167.5 0.2 slice.4183
  167.9 0.2 slice.4184
  168.0 0.2 pad_select_fusion.5
  168.2 0.2 slice.4185
  168.5 0.2 slice.4186
  168.7 0.2 pad_select_fusion.3
  168.8 0.2 slice.4187
  169.2 0.2 slice.4188
  169.5 0.2 pad_select_fusion
  169.8 1.9 collective-permute-start.11
  171.7 3.4 %collective-permute-start.12 = (bf16[10,4,4,128]{3,2,1,0:T(4,128)(2,1)S(1)}, bf16[10,4,4,128]{3,2,1,0:T(4,128)(2,1)S(1)}, u32[]{:S(2)}, u32[]{:S(2)}) collective-permute-start(bf16[10,4,4,128]{3,2,1,0:T(4,128)(2,1)S(1)} %get-tuple-element.17), channel_id=1, source_target_pairs={{64,0},{128,64},{192,128},{256,192},{320,256},{384,320},{448,384},... | collective-permute-start | bytes 122888 | tf_op jit(solution)/shard_map/ppermute | solution.py:24
  175.1 0.3 bitcast_multiply_fusion
  175.5 3.6 %collective-permute-done.12 = bf16[10,4,4,128]{3,2,1,0:T(4,128)(2,1)S(1)} collective-permute-done((bf16[10,4,4,128]{3,2,1,0:T(4,128)(2,1)S(1)}, bf16[10,4,4,128]{3,2,1,0:T(4,128)(2,1)S(1)}, u32[]{:S(2)}, u32[]{:S(2)}) %collective-permute-start.12) | collective-permute-done | bytes 40992 | tf_op jit(solution)/shard_map/ppermute | solution.py:24
  179.4 1.9 collective-permute-start.13
  181.3 7.0 %collective-permute-start.14 = (bf16[10,4,24,4]{3,2,1,0:T(8,128)(2,1)S(1)}, bf16[10,4,24,4]{3,2,1,0:T(8,128)(2,1)S(1)}, u32[]{:S(2)}, u32[]{:S(2)}) collective-permute-start(bf16[10,4,24,4]{3,2,1,0:T(8,128)(2,1)S(1)} %get-tuple-element.19), channel_id=1, source_target_pairs={{1,0},{2,1},{3,2},{4,3},{5,4},{6,5},{7,6},{8,7},{9,8},{10,9},{11,1... | collective-permute-start | bytes 23048 | tf_op jit(solution)/shard_map/ppermute | solution.py:24
  188.4 4.2 %collective-permute-done.13 = bf16[10,4,24,4]{3,2,1,0:T(8,128)(2,1)S(1)} collective-permute-done((bf16[10,4,24,4]{3,2,1,0:T(8,128)(2,1)S(1)}, bf16[10,4,24,4]{3,2,1,0:T(8,128)(2,1)S(1)}, u32[]{:S(2)}, u32[]{:S(2)}) %collective-permute-start.13) | collective-permute-done | bytes 7712 | tf_op jit(solution)/shard_map/ppermute | solution.py:21
  192.5 5.0 %collective-permute-done.14 = bf16[10,4,24,4]{3,2,1,0:T(8,128)(2,1)S(1)} collective-permute-done((bf16[10,4,24,4]{3,2,1,0:T(8,128)(2,1)S(1)}, bf16[10,4,24,4]{3,2,1,0:T(8,128)(2,1)S(1)}, u32[]{:S(2)}, u32[]{:S(2)}) %collective-permute-start.14) | collective-permute-done | bytes 7712 | tf_op jit(solution)/shard_map/ppermute | solution.py:24
  197.6 0.5 maximum_select_fusion
  198.1 44.1 %add_convert_fusion = bf16[10,4,16,128]{3,2,1,0:T(8,128)(2,1)} fusion(f32[4,16,128]{2,1,0:T(8,128)S(1)} %get-tuple-element.2, f32[4,16,128]{2,1,0:T(8,128)S(1)} %get-tuple-element.49, f32[4,16,128]{2,1,0:T(8,128)S(1)} %get-tuple-element.52, f32[4,16,128]{2,1,0:T(8,128)S(1)} %get-tuple-element.37, f32[4,16,128]{2,1,0:T(8,128)S(1)} %get-tuple-element.4, ...), kind=kLoop, calls=%fused_computation.592 | loop fusion | flops 145244160 | bytes 14811136 | tf_op jit(solution)/shard_map/convert_element_type | solution.py:145
  (35 shorter events, 2.0 us)
Async XLA Ops:
  0.6 12.2 %copy-start = (f32[3,4,16,128]{3,2,1,0:T(8,128)S(1)}, f32[3,4,16,128]{3,2,1,0:T(8,128)}, u32[]{:S(2)}) copy-start(f32[3,4,16,128]{3,2,1,0:T(8,128)} %param.4) | copy-start | bytes 294916
  1.5 11.3 %collective-permute-start = (f32[3,4,2,128]{3,2,1,0:T(2,128)S(1)}, f32[3,4,2,128]{3,2,1,0:T(2,128)S(1)}, u32[]{:S(2)}, u32[]{:S(2)}) collective-permute-start(f32[3,4,2,128]{3,2,1,0:T(2,128)S(1)} %get-tuple-element.98), channel_id=1, source_target_pairs={{0,64},{64,128},{128,192},{192,256},{256,320},{320,384},{384,448},... | collective-permute-start | bytes 36872 | tf_op jit(solution)/shard_map/ppermute | solution.py:21
  4.9 8.0 %collective-permute-start.1 = (f32[3,4,2,128]{3,2,1,0:T(2,128)S(1)}, f32[3,4,2,128]{3,2,1,0:T(2,128)S(1)}, u32[]{:S(2)}, u32[]{:S(2)}) collective-permute-start(f32[3,4,2,128]{3,2,1,0:T(2,128)S(1)} %get-tuple-element.99), channel_id=1, source_target_pairs={{64,0},{128,64},{192,128},{256,192},{320,256},{384,320},{448,384},... | collective-permute-start | bytes 36872 | tf_op jit(solution)/shard_map/ppermute | solution.py:24
  6.8 31.7 %collective-permute-start.4 = (bf16[10,4,16,128]{3,2,1,0:T(8,128)(2,1)}, bf16[10,4,16,128]{3,2,1,0:T(8,128)(2,1)S(1)}, u32[]{:S(2)}, u32[]{:S(2)}) collective-permute-start(bf16[10,4,16,128]{3,2,1,0:T(8,128)(2,1)} %param.3), channel_id=1, source_target_pairs={{0,1},{1,2},{2,3},{3,4},{4,5},{5,6},{6,7},{7,8},{8,9},{9,10},{10,1... | collective-permute-start | bytes 491528 | tf_op jit(solution)/shard_map/ppermute | solution.py:12
  13.0 25.5 %copy-start.2 = (bf16[10,4,16,128]{3,2,1,0:T(8,128)(2,1)S(1)}, bf16[10,4,16,128]{3,2,1,0:T(8,128)(2,1)}, u32[]{:S(2)}) copy-start(bf16[10,4,16,128]{3,2,1,0:T(8,128)(2,1)} %param.3) | copy-start | bytes 491524
  13.0 24.0 %collective-permute-start.2 = (f32[3,4,20,2]{3,2,1,0:T(8,128)S(1)}, f32[3,4,20,2]{3,2,1,0:T(8,128)S(1)}, u32[]{:S(2)}, u32[]{:S(2)}) collective-permute-start(f32[3,4,20,2]{3,2,1,0:T(8,128)S(1)} %get-tuple-element.20), channel_id=1, source_target_pairs={{0,1},{1,2},{2,3},{3,4},{4,5},{5,6},{6,7},{7,8},{8,9},{9,10},{10,1... | collective-permute-start | bytes 5768 | tf_op jit(solution)/shard_map/ppermute | solution.py:21
  16.9 21.3 %collective-permute-start.3 = (f32[3,4,20,2]{3,2,1,0:T(8,128)S(1)}, f32[3,4,20,2]{3,2,1,0:T(8,128)S(1)}, u32[]{:S(2)}, u32[]{:S(2)}) collective-permute-start(f32[3,4,20,2]{3,2,1,0:T(8,128)S(1)} %get-tuple-element.21), channel_id=1, source_target_pairs={{1,0},{2,1},{3,2},{4,3},{5,4},{6,5},{7,6},{8,7},{9,8},{10,9},{11,1... | collective-permute-start | bytes 5768 | tf_op jit(solution)/shard_map/ppermute | solution.py:24
  38.6 11.1 %collective-permute-start.5 = (bf16[10,4,16,128]{3,2,1,0:T(8,128)(2,1)S(1)}, bf16[10,4,16,128]{3,2,1,0:T(8,128)(2,1)S(1)}, u32[]{:S(2)}, u32[]{:S(2)}) collective-permute-start(bf16[10,4,16,128]{3,2,1,0:T(8,128)(2,1)S(1)} %broadcast_select_fusion), channel_id=1, source_target_pairs={{0,2},{1,3},{2,4},{3,5},{4,6},{5,7},{6,8},{7,9},{8,10},{9,11},{10,... | collective-permute-start | bytes 491528 | tf_op jit(solution)/shard_map/ppermute | solution.py:12
  49.8 12.3 %collective-permute-start.6 = (bf16[10,4,16,128]{3,2,1,0:T(8,128)(2,1)S(1)}, bf16[10,4,16,128]{3,2,1,0:T(8,128)(2,1)S(1)}, u32[]{:S(2)}, u32[]{:S(2)}) collective-permute-start(bf16[10,4,16,128]{3,2,1,0:T(8,128)(2,1)S(1)} %broadcast_select_fusion.1), channel_id=1, source_target_pairs={{0,4},{1,5},{2,6},{3,7},{4,8},{5,9},{6,10},{7,11},{8,12},{9,13},{1... | collective-permute-start | bytes 491528 | tf_op jit(solution)/shard_map/ppermute | solution.py:12
  62.3 20.3 %collective-permute-start.7 = (bf16[10,4,16,128]{3,2,1,0:T(8,128)(2,1)S(1)}, bf16[10,4,16,128]{3,2,1,0:T(8,128)(2,1)S(1)}, u32[]{:S(2)}, u32[]{:S(2)}) collective-permute-start(bf16[10,4,16,128]{3,2,1,0:T(8,128)(2,1)S(1)} %broadcast_select_fusion.2), channel_id=1, source_target_pairs={{0,8},{1,9},{2,10},{3,11},{4,12},{5,13},{6,14},{7,15},{8,16},{9,17... | collective-permute-start | bytes 491528 | tf_op jit(solution)/shard_map/ppermute | solution.py:12
  82.6 33.0 %collective-permute-start.8 = (bf16[10,4,16,128]{3,2,1,0:T(8,128)(2,1)S(1)}, bf16[10,4,16,128]{3,2,1,0:T(8,128)(2,1)S(1)}, u32[]{:S(2)}, u32[]{:S(2)}) collective-permute-start(bf16[10,4,16,128]{3,2,1,0:T(8,128)(2,1)S(1)} %broadcast_select_fusion.3), channel_id=1, source_target_pairs={{0,16},{1,17},{2,18},{3,19},{4,20},{5,21},{6,22},{7,23},{8,24},{9,... | collective-permute-start | bytes 491528 | tf_op jit(solution)/shard_map/ppermute | solution.py:12
  115.7 40.6 %collective-permute-start.9 = (bf16[10,4,16,128]{3,2,1,0:T(8,128)(2,1)S(1)}, bf16[10,4,16,128]{3,2,1,0:T(8,128)(2,1)S(1)}, u32[]{:S(2)}, u32[]{:S(2)}) collective-permute-start(bf16[10,4,16,128]{3,2,1,0:T(8,128)(2,1)S(1)} %broadcast_select_fusion.4), channel_id=1, source_target_pairs={{0,32},{1,33},{2,34},{3,35},{4,36},{5,37},{6,38},{7,39},{8,40},{9,... | collective-permute-start | bytes 491528 | tf_op jit(solution)/shard_map/ppermute | solution.py:12
  131.4 56.9 %copy-start.1 = (f32[3,4,16,128]{3,2,1,0:T(8,128)}, f32[3,4,16,128]{3,2,1,0:T(8,128)S(1)}, u32[]{:S(2)}) copy-start(f32[3,4,16,128]{3,2,1,0:T(8,128)S(1)} %multiply_add_fusion.4) | copy-start | bytes 294916
  156.5 10.7 %collective-permute-start.10 = (bf16[10,4,16,128]{3,2,1,0:T(8,128)(2,1)S(1)}, bf16[10,4,16,128]{3,2,1,0:T(8,128)(2,1)S(1)}, u32[]{:S(2)}, u32[]{:S(2)}) collective-permute-start(bf16[10,4,16,128]{3,2,1,0:T(8,128)(2,1)S(1)} %broadcast_select_fusion.5), channel_id=1, source_target_pairs={{0,1},{1,2},{2,3},{3,4},{4,5},{5,6},{6,7},{7,8},{8,9},{9,10},{10,1... | collective-permute-start | bytes 491528 | tf_op jit(solution)/shard_map/ppermute | solution.py:12
  169.8 5.7 %collective-permute-start.11 = (bf16[10,4,4,128]{3,2,1,0:T(4,128)(2,1)S(1)}, bf16[10,4,4,128]{3,2,1,0:T(4,128)(2,1)S(1)}, u32[]{:S(2)}, u32[]{:S(2)}) collective-permute-start(bf16[10,4,4,128]{3,2,1,0:T(4,128)(2,1)S(1)} %get-tuple-element.16), channel_id=1, source_target_pairs={{0,64},{64,128},{128,192},{192,256},{256,320},{320,384},{384,448},... | collective-permute-start | bytes 122888 | tf_op jit(solution)/shard_map/ppermute | solution.py:21
  171.7 7.4 %collective-permute-start.12 = (bf16[10,4,4,128]{3,2,1,0:T(4,128)(2,1)S(1)}, bf16[10,4,4,128]{3,2,1,0:T(4,128)(2,1)S(1)}, u32[]{:S(2)}, u32[]{:S(2)}) collective-permute-start(bf16[10,4,4,128]{3,2,1,0:T(4,128)(2,1)S(1)} %get-tuple-element.17), channel_id=1, source_target_pairs={{64,0},{128,64},{192,128},{256,192},{320,256},{384,320},{448,384},... | collective-permute-start | bytes 122888 | tf_op jit(solution)/shard_map/ppermute | solution.py:24
  179.4 13.1 %collective-permute-start.13 = (bf16[10,4,24,4]{3,2,1,0:T(8,128)(2,1)S(1)}, bf16[10,4,24,4]{3,2,1,0:T(8,128)(2,1)S(1)}, u32[]{:S(2)}, u32[]{:S(2)}) collective-permute-start(bf16[10,4,24,4]{3,2,1,0:T(8,128)(2,1)S(1)} %get-tuple-element.18), channel_id=1, source_target_pairs={{0,1},{1,2},{2,3},{3,4},{4,5},{5,6},{6,7},{7,8},{8,9},{9,10},{10,1... | collective-permute-start | bytes 23048 | tf_op jit(solution)/shard_map/ppermute | solution.py:21
  181.3 16.2 %collective-permute-start.14 = (bf16[10,4,24,4]{3,2,1,0:T(8,128)(2,1)S(1)}, bf16[10,4,24,4]{3,2,1,0:T(8,128)(2,1)S(1)}, u32[]{:S(2)}, u32[]{:S(2)}) collective-permute-start(bf16[10,4,24,4]{3,2,1,0:T(8,128)(2,1)S(1)} %get-tuple-element.19), channel_id=1, source_target_pairs={{1,0},{2,1},{3,2},{4,3},{5,4},{6,5},{7,6},{8,7},{9,8},{10,9},{11,1... | collective-permute-start | bytes 23048 | tf_op jit(solution)/shard_map/ppermute | solution.py:24
where the time goes:
time: 243 us; the launch traced here: 242 us
  waiting for transfers between devices  115 us (47%)
  starting transfers between devices  69 us (28%)
  other arithmetic  55.1 us (23%)
    ppermute x7, waiting for transfers between devices, shifted_2(): lax.ppermute(x, axis, [(i, (i + by) % length) for i in range(length)])  98.5 us
    convert_element_type x1, other arithmetic, local(): return (result.astype(jnp.bfloat16), disp)  44.1 us
    ppermute x4, starting transfers between devices, padded(): lax.ppermute(lax.slice_in_dim(block, 0, width, axis=dim), axis, backward)  30.1 us
    ppermute x7, starting transfers between devices, shifted_2(): lax.ppermute(x, axis, [(i, (i + by) % length) for i in range(length)])  27.8 us
    ppermute x4, starting transfers between devices, padded(): lax.ppermute(lax.slice_in_dim(block, block.shape[dim] - width, None, axis...  11.1 us
    ppermute x4, waiting for transfers between devices, padded(): lax.ppermute(lax.slice_in_dim(block, 0, width, axis=dim), axis, backward)  9.95 us
    ppermute x4, waiting for transfers between devices, padded(): lax.ppermute(lax.slice_in_dim(block, block.shape[dim] - width, None, axis...  6.36 us
    add x3, other arithmetic, local(): total = total + wind_z_weights[wind_iz] * wind_plane  5.55 us
  transfers between devices with their start and end apart: 15, of which 11 were waited for; matrix products, arithmetic and copies ran while one was open for 3% of the time, Pallas kernels for 0%

commit v1 on v0

v1 whole, which is shorter than its diff:
```python
import jax
import jax.numpy as jnp
from jax import lax
from jax.experimental import pallas as pl
from jax.experimental.pallas import tpu as pltpu
from jax.sharding import PartitionSpec as P


ITERS = 3
RIM = 4
LANES = 128
SPAN = 9


def ring_shift(x, axis, by):
    length = lax.axis_size(axis)
    return lax.ppermute(x, axis, [(i, (i + by) % length) for i in range(length)])


def padded(block, sides, width):
    for axis, dim in sides:
        low = ring_shift(lax.slice_in_dim(block, block.shape[dim] - width, None, axis=dim), axis, 1)
        high = ring_shift(lax.slice_in_dim(block, 0, width, axis=dim), axis, -1)
        block = jnp.concatenate([low, block, high], axis=dim)
    return block


def cubic_weights(frac):
    return (
        -frac * (frac - 1.0) * (frac - 2.0) / 6.0,
        (frac + 1.0) * (frac - 1.0) * (frac - 2.0) / 2.0,
        -(frac + 1.0) * frac * (frac - 2.0) / 2.0,
        (frac + 1.0) * frac * (frac - 1.0) / 6.0,
    )


def spread(base, weights, lowest, highest):
    listed = []
    for target in range(lowest, highest + 1):
        summed = jnp.zeros(base.shape, jnp.float32)
        for a in range(len(weights)):
            summed = summed + jnp.where(base + a == target, weights[a], 0.0)
        listed.append(summed)
    return listed


def pole_zero(block, width, anchor, total_rows):
    rowpos = lax.broadcasted_iota(jnp.int32, (block.shape[2], 1), 0) + anchor - width
    keep = (rowpos >= 0) & (rowpos < total_rows)
    return jnp.where(keep, block, jnp.zeros_like(block))


def trajectory(winds, anchor, total_rows):
    _, levels, rows, cols = winds.shape
    shape = (levels, rows, cols)
    kpos = lax.broadcasted_iota(jnp.float32, shape, 0)
    kint = lax.broadcasted_iota(jnp.int32, shape, 0)
    growi = lax.broadcasted_iota(jnp.int32, shape, 1) + anchor
    gpos = growi.astype(jnp.float32)
    wide = padded(winds, (("lon", 3), ("lat", 2)), 2)
    wide = pole_zero(wide, 2, anchor, total_rows)
    wide = jnp.pad(wide, ((0, 0), (2, 2), (0, 0), (0, 0)))
    disp = winds
    for _ in range(ITERS):
        zlev = jnp.clip(kpos - 0.5 * disp[0], 0.0, levels - 1.0)
        ylat = jnp.clip(gpos - 0.5 * disp[1], 0.0, total_rows - 1.0)
        xrel = -0.5 * disp[2]
        zb = jnp.floor(zlev)
        yb = jnp.floor(ylat)
        xb = jnp.floor(xrel)
        tz = zlev - zb
        ty = ylat - yb
        tx = xrel - xb
        z_weights = spread(zb.astype(jnp.int32) - kint, (1.0 - tz, tz), -2, 2)
        y_weights = spread(yb.astype(jnp.int32) - growi, (1.0 - ty, ty), -2, 2)
        x_weights = spread(xb.astype(jnp.int32), (1.0 - tx, tx), -2, 2)
        total = jnp.zeros((3,) + shape, jnp.float32)
        for iz in range(5):
            plane = jnp.zeros((3,) + shape, jnp.float32)
            for iy in range(5):
                line = jnp.zeros((3,) + shape, jnp.float32)
                for ix in range(5):
                    line = line + x_weights[ix] * wide[:, iz : iz + levels, iy : iy + rows, ix : ix + cols]
                plane = plane + y_weights[iy] * line
            total = total + z_weights[iz] * plane
        disp = total
    return disp


def lane_pick(x, index):
    return jnp.take_along_axis(x, index, axis=1)


def iota2(dim):
    return lax.broadcasted_iota(jnp.int32, (8, LANES), dim)


def prepare(tracers, shifts, westward, sectors):
    ntrac, levels, rows, cols = tracers.shape
    height = ntrac * rows + 16

    def body(west_ref, shift_ref, in_ref, out_ref, hop_ref, rim_ref):
        lane = iota2(1)
        sub = iota2(0)
        picks, hops, places = [], [], []
        edge = jnp.where((lane & 7) < RIM, cols - RIM + (lane & 7), (lane & 7) - RIM)
        step = jnp.where((lane & 7) < RIM, 1, -1)
        rim_hops = jnp.zeros((1, LANES), jnp.float32)
        for g in range(rows // 8):
            total = shift_ref[8 * g : 8 * g + 8, :]
            within = total & (cols - 1)
            picks.append((lane - within) & (cols - 1))
            hop = (total >> 7) + jnp.where(lane < within, 1, 0)
            hops.append(hop)
            places.append((lane >> 3) == sub + 8 * g)
            edge_hop = lane_pick(hop.astype(jnp.float32), edge)
            rim_hops = rim_hops + jnp.sum(jnp.where(places[g], edge_hop, 0.0), axis=0, keepdims=True)
        rim_hop = jnp.broadcast_to(rim_hops, (8, LANES)).astype(jnp.int32) + step
        hops = [jnp.where(west_ref[0] == 1, -hop, hop) & (sectors - 1) for hop in hops + [rim_hop]]
        for t in range(ntrac):
            for g in range(rows // 8):
                hop_ref[t * rows + 8 * g : t * rows + 8 * g + 8, :] = hops[g]
        hop_ref[height - 16 : height - 8, :] = hops[-1]
        hop_ref[height - 8 : height, :] = hops[-1]
        rim_ref[...] = jnp.zeros_like(rim_ref)

        def level(k, carry):
            for t in range(ntrac):
                block = in_ref[t, k].astype(jnp.float32)
                turned = []
                rim = jnp.zeros((8, LANES), jnp.float32)
                for g in range(rows // 8):
                    part = lane_pick(block[8 * g : 8 * g + 8], picks[g])
                    turned.append(part)
                    rim = rim + jnp.where(places[g], lane_pick(part, edge), 0.0)
                out_ref[k, t * rows : (t + 1) * rows, :] = jnp.concatenate(turned, axis=0).astype(jnp.bfloat16)
                rim_ref[t : t + 1, :] = jnp.sum(rim, axis=0, keepdims=True)
            out_ref[k, height - 16 : height, :] = rim_ref[...].astype(jnp.bfloat16)
            return carry

        lax.fori_loop(0, levels, level, 0)

    smem = pl.BlockSpec(memory_space=pltpu.SMEM)
    vmem = pl.BlockSpec(memory_space=pltpu.VMEM)
    return pl.pallas_call(
        body,
        out_shape=(
            jax.ShapeDtypeStruct((levels, height, LANES), jnp.bfloat16),
            jax.ShapeDtypeStruct((height, LANES), jnp.int32),
        ),
        in_specs=[smem, vmem, vmem],
        scratch_shapes=[pltpu.VMEM((16, LANES), jnp.float32)],
        name="prepare",
    )(westward, shifts, tracers)


def edges_of(main, ntrac, rows):
    levels, height, _ = main.shape
    cut = -(-ntrac * RIM // 8) * 8

    def body(main_ref, first_ref, last_ref, a_ref, b_ref):
        a_ref[...] = jnp.zeros_like(a_ref)
        b_ref[...] = jnp.zeros_like(b_ref)
        for k in range(levels):
            for t in range(ntrac):
                block = main_ref[k, t * rows : (t + 1) * rows, :].astype(jnp.float32)
                a_ref[t * RIM : (t + 1) * RIM, :] = block[:RIM]
                b_ref[t * RIM : (t + 1) * RIM, :] = block[rows - RIM :]
            rim = main_ref[k, height - 16 : height, :]
            first_ref[k, :cut, :] = a_ref[...].astype(jnp.bfloat16)
            last_ref[k, :cut, :] = b_ref[...].astype(jnp.bfloat16)
            first_ref[k, cut:, :] = rim
            last_ref[k, cut:, :] = rim

    edge = jax.ShapeDtypeStruct((levels, cut + 16, LANES), jnp.bfloat16)
    return pl.pallas_call(
        body,
        out_shape=(edge, edge),
        scratch_shapes=[pltpu.VMEM((cut, LANES), jnp.float32), pltpu.VMEM((cut, LANES), jnp.float32)],
        name="edges_of",
    )(main)


def interpolate(place, disp, main, below, above, ntrac, rows, total_rows):
    levels = main.shape[0]
    height = ntrac * rows + 16
    groups = rows // 8
    tall = rows + 2 * RIM
    weight_count = 2 * SPAN + levels
    cut = ntrac * RIM

    def body(
        place_ref, disp_ref, main_ref, below_ref, above_ref, out_ref, weight_ref, rim_ref, end_ref, even_ref, odd_ref
    ):
        lane = iota2(1)
        sub = iota2(0)
        anchor = place_ref[0]
        has_below = place_ref[0] > 0
        has_above = place_ref[0] + rows < total_rows

        def weigh(k, carry):
            for g in range(groups):
                at = pl.ds(8 * g, 8)
                row_index = sub + (8 * g) + anchor
                zdep = jnp.clip(k.astype(jnp.float32) - disp_ref[0, k, at, :], 0.0, levels - 1.0)
                ydep = jnp.clip(row_index.astype(jnp.float32) - disp_ref[1, k, at, :], 0.0, total_rows - 1.0)
                xrel = -disp_ref[2, k, at, :]
                zb = jnp.floor(zdep)
                yb = jnp.floor(ydep)
                xb = jnp.floor(xrel)
                x_weights = spread(xb.astype(jnp.int32) - 1, cubic_weights(xrel - xb), -4, 4)
                y_weights = spread(yb.astype(jnp.int32) - row_index - 1, cubic_weights(ydep - yb), -4, 4)
                z_weights = spread(zb.astype(jnp.int32) - 1, cubic_weights(zdep - zb), 0, levels - 1)
                for n, value in enumerate(x_weights + y_weights + z_weights):
                    weight_ref[(k * groups + g) * weight_count + n] = value
            return carry

        lax.fori_loop(0, levels, weigh, 0)

        for l in range(levels):
            rim_ref[l, 0] = main_ref[l, height - 16 : height, :].astype(jnp.float32)
            rim_ref[l, 1] = jnp.where(has_below, below_ref[l, cut:, :].astype(jnp.float32), 0.0)
            rim_ref[l, 2] = jnp.where(has_above, above_ref[l, cut:, :].astype(jnp.float32), 0.0)
            end_ref[l, 0] = jnp.where(has_below, below_ref[l, :cut, :].astype(jnp.float32), 0.0)
            end_ref[l, 1] = jnp.where(has_above, above_ref[l, :cut, :].astype(jnp.float32), 0.0)

        near = (lane + RIM) & 7

        def build(t, to_ref):
            base = pl.multiple_of(t * rows, rows)
            for l in range(levels):
                own = jnp.broadcast_to(rim_ref[l, 0, pl.ds(t, 1), :], (8, LANES))
                block = main_ref[l, pl.ds(base, rows), :].astype(jnp.float32)
                ends = [end_ref[l, n, pl.ds(t * RIM, RIM), :] for n in range(2)]
                block = jnp.concatenate([ends[0], block, ends[1]], axis=0)
                lower = jnp.broadcast_to(rim_ref[l, 1, pl.ds(t, 1), :], (8, LANES))
                upper = jnp.broadcast_to(rim_ref[l, 2, pl.ds(t, 1), :], (8, LANES))
                for v in range(tall // 8):
                    inner_row = sub + (8 * v - RIM)
                    source = own
                    if v == 0:
                        source = jnp.where(sub < RIM, lower, own)
                    if v == tall // 8 - 1:
                        source = jnp.where(sub >= RIM, upper, own)
                    edges = lane_pick(source, ((inner_row & (rows - 1)) << 3) + near)
                    middle = block[8 * v : 8 * v + 8]
                    for ix in range(SPAN):
                        o = ix - RIM
                        if o > 0:
                            value = pltpu.roll(jnp.where(lane < o, edges, middle), LANES - o, 1)
                        elif o < 0:
                            value = pltpu.roll(jnp.where(lane >= LANES + o, edges, middle), -o, 1)
                        else:
                            value = middle
                        to_ref[l * SPAN + ix, 8 * v : 8 * v + 8, :] = value

        def cells(t, kp, from_ref):
            results = [[], []]
            for g in range(groups):
                at = [((2 * kp + h) * groups + g) * weight_count for h in range(2)]
                wx = [[weight_ref[at[h] + n] for n in range(SPAN)] for h in range(2)]
                result = [None, None]
                for l in range(levels):
                    plane = [None, None]
                    for iy in range(SPAN):
                        line = [None, None]
                        first = 8 * g + iy
                        for ix in range(SPAN):
                            value = from_ref[l * SPAN + ix, first : first + 8, :]
                            for h in range(2):
                                term = wx[h][ix] * value
                                line[h] = term if ix == 0 else line[h] + term
                        for h in range(2):
                            term = weight_ref[at[h] + SPAN + iy] * line[h]
                            plane[h] = term if plane[h] is None else plane[h] + term
                    for h in range(2):
                        term = weight_ref[at[h] + 2 * SPAN + l] * plane[h]
                        result[h] = term if l == 0 else result[h] + term
                for h in range(2):
                    results[h].append(result[h])
            for h in range(2):
                out_ref[t, 2 * kp + h] = jnp.concatenate(results[h], axis=0).astype(jnp.bfloat16)

        build(0, even_ref)

        def tracers(pair, carry):
            t = 2 * pair
            build(t + 1, odd_ref)
            for kp in range(levels // 2):
                cells(t, kp, even_ref)
            build(jnp.minimum(t + 2, ntrac - 1), even_ref)
            for kp in range(levels // 2):
                cells(t + 1, kp, odd_ref)
            return carry

        lax.fori_loop(0, ntrac // 2, tracers, 0)

    smem = pl.BlockSpec(memory_space=pltpu.SMEM)
    vmem = pl.BlockSpec(memory_space=pltpu.VMEM)
    return pl.pallas_call(
        body,
        out_shape=jax.ShapeDtypeStruct((ntrac, levels, rows, LANES), jnp.bfloat16),
        in_specs=[smem] + [vmem] * 4,
        scratch_shapes=[
            pltpu.VMEM((levels * groups * weight_count, 8, LANES), jnp.float32),
            pltpu.VMEM((levels, 3, 16, LANES), jnp.float32),
            pltpu.VMEM((levels, 2, cut, LANES), jnp.float32),
            pltpu.VMEM((levels * SPAN, tall, LANES), jnp.float32),
            pltpu.VMEM((levels * SPAN, tall, LANES), jnp.float32),
        ],
        name="interpolate",
    )(place, disp, main, below, above)


def parity_shift(x, by):
    tall = lax.axis_size("lat")
    wide = lax.axis_size("lon")
    pairs = []
    for a in range(tall):
        way = -by if a & 1 else by
        pairs += [(a * wide + b, a * wide + (b + way) % wide) for b in range(wide)]
    return lax.ppermute(x, ("lat", "lon"), pairs)


def local(tracers, winds, zonal_shift):
    ntrac, _, rows, _ = tracers.shape
    sectors = lax.axis_size("lon")
    total_rows = rows * lax.axis_size("lat")
    anchor = lax.axis_index("lat") * rows
    place = anchor.reshape(1)
    shifts = jnp.broadcast_to(zonal_shift[:, None], (rows, LANES))
    odd = lax.axis_index("lat") & 1
    main, hops = prepare(tracers, shifts, odd.reshape(1), sectors)
    for bit in range(sectors.bit_length() - 1):
        moved = parity_shift(main, 1 << bit)
        main = jnp.where((hops >> bit & 1) == 1, moved, main)
    disp = trajectory(winds, anchor, total_rows)
    first, last = edges_of(main, ntrac, rows)
    below = ring_shift(last, "lat", 1)
    above = ring_shift(first, "lat", -1)
    new = interpolate(place, disp, main, below, above, ntrac, rows, total_rows)
    return new, disp


def solution(mesh):
    return jax.shard_map(
        local,
        mesh=mesh,
        in_specs=(P(None, None, "lat", "lon"), P(None, None, "lat", "lon"), P("lat")),
        out_specs=(P(None, None, "lat", "lon"), P(None, None, "lat", "lon")),
        check_vma=False,
    )
```

time: 243 us -> 171 us (0.70)
  waiting for transfers between devices: 115 us -> 67.1 us
  other arithmetic: 55.1 us -> 8.77 us
  Pallas kernels: 0 us -> 17.6 us
  starting transfers between devices: 69 us -> 72.9 us
    ppermute x15 -> x12, waiting for transfers between devices: 115 us -> 67.1 us  [the longest x6 64.3 us: parity_shift(): return lax.ppermute(x, ('lat', 'lon'), pairs)]
    convert_element_type x1 -> x0, other arithmetic: 44.1 us -> none  [local(): return (result.astype(jnp.bfloat16), disp)]
    pallas_call x0 -> x3, Pallas kernels: none -> 17.6 us  [the longest x1 13.6 us: interpolate(): pl.pallas_call(body, out_shape=jax.ShapeDtypeStruct((ntrac, levels, rows,...]
    ppermute x15 -> x12, starting transfers between devices: 69 us -> 72.9 us  [the longest x6 37.9 us: parity_shift(): return lax.ppermute(x, ('lat', 'lon'), pairs)]
  transfers between devices with their start and end apart: 15 -> 12, of which waited for: 11 -> 6; matrix products, arithmetic and copies ran while one was open for 3% -> 5% of each run, Pallas kernels for 0% -> 1%
where the time goes in v1:
time: 171 us; the launch traced here: 170 us
  starting transfers between devices  72.9 us (43%)
  waiting for transfers between devices  67.1 us (39%)
  Pallas kernels  17.6 us (10%)
  other arithmetic  8.77 us (5%)
  local copies, waits for them, and re-layouts  3 us (2%)
    ppermute x6, waiting for transfers between devices, parity_shift(): return lax.ppermute(x, ('lat', 'lon'), pairs)  64.3 us
    ppermute x6, starting transfers between devices, parity_shift(): return lax.ppermute(x, ('lat', 'lon'), pairs)  37.9 us
    ppermute x6, starting transfers between devices, ring_shift(): lax.ppermute(x, axis, [(i, (i + by) % length) for i in range(length)])  35 us
    pallas_call x1, Pallas kernels, interpolate(): pl.pallas_call(body, out_shape=jax.ShapeDtypeStruct((ntrac, levels, rows,...  13.6 us
    add x3, other arithmetic, trajectory(): total = total + z_weights[iz] * plane  6.19 us
  transfers between devices with their start and end apart: 12, of which 6 were waited for; matrix products, arithmetic and copies ran while one was open for 5% of the time, Pallas kernels for 1%

profile of v1, /device:TPU:25, one launch (start us, length us, event | category | flops | bytes accessed | tf_op | source)
XLA Modules:
  0.0 170.3 jit_solution(17932814587708622640)
XLA Ops:
  0.6 1.1 fusion.15
  1.7 20.9 %collective-permute-start.1 = (f32[3,4,16,2]{3,2,1,0:T(8,128)S(1)}, f32[3,4,16,2]{3,2,1,0:T(8,128)S(1)}, u32[]{:S(2)}, u32[]{:S(2)}) collective-permute-start(f32[3,4,16,2]{3,2,1,0:T(8,128)S(1)} %get-tuple-element.73), channel_id=1, source_target_pairs={{0,63},{1,0},{2,1},{3,2},{4,3},{5,4},{6,5},{7,6},{8,7},{9,8},{10,9... | collective-permute-start | bytes 4616 | tf_op jit(solution)/shard_map/ppermute | solution.py:17
  22.6 1.9 %collective-permute-start = (f32[3,4,16,2]{3,2,1,0:T(8,128)S(1)}, f32[3,4,16,2]{3,2,1,0:T(8,128)S(1)}, u32[]{:S(2)}, u32[]{:S(2)}) collective-permute-start(f32[3,4,16,2]{3,2,1,0:T(8,128)S(1)} %get-tuple-element.72), channel_id=1, source_target_pairs={{0,1},{1,2},{2,3},{3,4},{4,5},{5,6},{6,7},{7,8},{8,9},{9,10},{10,1... | collective-permute-start | bytes 4616 | tf_op jit(solution)/shard_map/ppermute | solution.py:17
  24.5 0.0 copy-start.4
  24.5 0.6 copy-done.4
  25.1 0.7 broadcast_in_dim.124.shift_ref
  25.8 2.4 %prepare.1 = (bf16[4,176,128]{2,1,0:T(8,128)(2,1)}, s32[176,128]{1,0:T(8,128)}) custom-call(s32[1]{0:T(128)} %bitcast.46.west_ref, s32[16,128]{1,0:T(8,128)} %broadcast_in_dim.124.shift_ref, bf16[10,4,16,128]{3,2,1,0:T(8,128)(2,1)} %in_ref.1), custom_call_target="tpu_custom_call" | custom-call | tf_op jit(solution)/shard_map/prepare/pallas_call | solution.py:145
  28.2 7.0 %collective-permute-start.4 = (bf16[4,176,128]{2,1,0:T(8,128)(2,1)}, bf16[4,176,128]{2,1,0:T(8,128)(2,1)S(1)}, u32[]{:S(2)}, u32[]{:S(2)}) collective-permute-start(bf16[4,176,128]{2,1,0:T(8,128)(2,1)} %get-tuple-element.7), channel_id=1, source_target_pairs={{0,1},{1,2},{2,3},{3,4},{4,5},{5,6},{6,7},{7,8},{8,9},{9,10},{10,1... | collective-permute-start | bytes 540680 | tf_op jit(solution)/shard_map/ppermute | solution.py:322
  35.2 0.0 copy-start
  35.2 1.0 and_compare_fusion.5
  36.3 0.0 copy-done
  36.3 0.1 add_bitcast_fusion.44
  36.4 0.0 copy-start.1
  36.4 0.0 collective-permute-done.1
  36.4 0.0 collective-permute-done
  36.5 0.1 pad_maximum_fusion.2
  36.6 1.9 %collective-permute-start.3 = (f32[3,4,2,132]{3,2,1,0:T(2,128)S(1)}, f32[3,4,2,132]{3,2,1,0:T(2,128)S(1)}, u32[]{:S(2)}, u32[]{:S(2)}) collective-permute-start(f32[3,4,2,132]{3,2,1,0:T(2,128)S(1)} %get-tuple-element.11), channel_id=1, source_target_pairs={{0,960},{64,0},{128,64},{192,128},{256,192},{320,256},{384,320},{4... | collective-permute-start | bytes 38024 | tf_op jit(solution)/shard_map/ppermute | solution.py:17
  38.5 5.8 %collective-permute-start.2 = (f32[3,4,2,132]{3,2,1,0:T(2,128)S(1)}, f32[3,4,2,132]{3,2,1,0:T(2,128)S(1)}, u32[]{:S(2)}, u32[]{:S(2)}) collective-permute-start(f32[3,4,2,132]{3,2,1,0:T(2,128)S(1)} %get-tuple-element.10), channel_id=1, source_target_pairs={{0,64},{64,128},{128,192},{192,256},{256,320},{320,384},{384,448},... | collective-permute-start | bytes 38024 | tf_op jit(solution)/shard_map/ppermute | solution.py:17
  44.3 0.0 collective-permute-done.4
  44.3 0.0 copy-done.1
  44.4 1.9 %collective-permute-start.5 = (bf16[4,176,128]{2,1,0:T(8,128)(2,1)S(1)}, bf16[4,176,128]{2,1,0:T(8,128)(2,1)S(1)}, u32[]{:S(2)}, u32[]{:S(2)}) collective-permute-start(bf16[4,176,128]{2,1,0:T(8,128)(2,1)S(1)} %broadcast_select_fusion), channel_id=1, source_target_pairs={{0,2},{1,3},{2,4},{3,5},{4,6},{5,7},{6,8},{7,9},{8,10},{9,11},{10,... | collective-permute-start | bytes 540680 | tf_op jit(solution)/shard_map/ppermute | solution.py:322
  46.3 0.0 collective-permute-done.3
  46.3 0.0 collective-permute-done.2
  46.3 0.2 maximum_select_fusion
  46.5 4.1 %collective-permute-done.5 = bf16[4,176,128]{2,1,0:T(8,128)(2,1)S(1)} collective-permute-done((bf16[4,176,128]{2,1,0:T(8,128)(2,1)S(1)}, bf16[4,176,128]{2,1,0:T(8,128)(2,1)S(1)}, u32[]{:S(2)}, u32[]{:S(2)}) %collective-permute-start.5) | collective-permute-done | bytes 180256 | tf_op jit(solution)/shard_map/ppermute | solution.py:322
  50.6 1.9 %collective-permute-start.6 = (bf16[4,176,128]{2,1,0:T(8,128)(2,1)S(1)}, bf16[4,176,128]{2,1,0:T(8,128)(2,1)S(1)}, u32[]{:S(2)}, u32[]{:S(2)}) collective-permute-start(bf16[4,176,128]{2,1,0:T(8,128)(2,1)S(1)} %broadcast_select_fusion.1), channel_id=1, source_target_pairs={{0,4},{1,5},{2,6},{3,7},{4,8},{5,9},{6,10},{7,11},{8,12},{9,13},{1... | collective-permute-start | bytes 540680 | tf_op jit(solution)/shard_map/ppermute | solution.py:322
  52.5 1.8 %multiply_add_fusion.2 = f32[3,4,16,128]{3,2,1,0:T(8,128)S(1)} fusion(f32[3,4,20,132]{3,2,1,0:T(8,128)S(1)} %maximum_select_fusion, f32[4,16,128]{2,1,0:T(8,128)S(1)} %get-tuple-element.64, f32[4,16,128]{2,1,0:T(8,128)S(1)} %get-tuple-element.60, f32[4,16,128]{2,1,0:T(8,128)S(1)} %get-tuple-element.59, f32[4,16,128]{2,1,0:T(8,128)S(1)} %get-tuple-element.58, ...), kind=kLoop, calls=%fused_computation.109 | loop fusion | flops 6856704 | bytes 3342336 | tf_op jit(solution)/shard_map/add | solution.py:85
  54.4 4.9 %collective-permute-done.6 = bf16[4,176,128]{2,1,0:T(8,128)(2,1)S(1)} collective-permute-done((bf16[4,176,128]{2,1,0:T(8,128)(2,1)S(1)}, bf16[4,176,128]{2,1,0:T(8,128)(2,1)S(1)}, u32[]{:S(2)}, u32[]{:S(2)}) %collective-permute-start.6) | collective-permute-done | bytes 180256 | tf_op jit(solution)/shard_map/ppermute | solution.py:322
  59.3 5.3 %collective-permute-start.7 = (bf16[4,176,128]{2,1,0:T(8,128)(2,1)S(1)}, bf16[4,176,128]{2,1,0:T(8,128)(2,1)S(1)}, u32[]{:S(2)}, u32[]{:S(2)}) collective-permute-start(bf16[4,176,128]{2,1,0:T(8,128)(2,1)S(1)} %broadcast_select_fusion.2), channel_id=1, source_target_pairs={{0,8},{1,9},{2,10},{3,11},{4,12},{5,13},{6,14},{7,15},{8,16},{9,17... | collective-permute-start | bytes 540680 | tf_op jit(solution)/shard_map/ppermute | solution.py:322
  64.6 0.1 add_bitcast_fusion.29
  64.8 7.9 %collective-permute-done.7 = bf16[4,176,128]{2,1,0:T(8,128)(2,1)S(1)} collective-permute-done((bf16[4,176,128]{2,1,0:T(8,128)(2,1)S(1)}, bf16[4,176,128]{2,1,0:T(8,128)(2,1)S(1)}, u32[]{:S(2)}, u32[]{:S(2)}) %collective-permute-start.7) | collective-permute-done | bytes 180256 | tf_op jit(solution)/shard_map/ppermute | solution.py:322
  72.7 7.5 %collective-permute-start.8 = (bf16[4,176,128]{2,1,0:T(8,128)(2,1)S(1)}, bf16[4,176,128]{2,1,0:T(8,128)(2,1)S(1)}, u32[]{:S(2)}, u32[]{:S(2)}) collective-permute-start(bf16[4,176,128]{2,1,0:T(8,128)(2,1)S(1)} %broadcast_select_fusion.3), channel_id=1, source_target_pairs={{0,16},{1,17},{2,18},{3,19},{4,20},{5,21},{6,22},{7,23},{8,24},{9,... | collective-permute-start | bytes 540680 | tf_op jit(solution)/shard_map/ppermute | solution.py:322
  80.2 1.8 %multiply_add_fusion.1 = f32[3,4,16,128]{3,2,1,0:T(8,128)S(1)} fusion(f32[3,4,20,132]{3,2,1,0:T(8,128)S(1)} %maximum_select_fusion, f32[4,16,128]{2,1,0:T(8,128)S(1)} %get-tuple-element.49, f32[4,16,128]{2,1,0:T(8,128)S(1)} %get-tuple-element.45, f32[4,16,128]{2,1,0:T(8,128)S(1)} %get-tuple-element.44, f32[4,16,128]{2,1,0:T(8,128)S(1)} %get-tuple-element.43, ...), kind=kLoop, calls=%fused_computation.108 | loop fusion | flops 6856704 | bytes 3342336 | tf_op jit(solution)/shard_map/add | solution.py:85
  82.1 12.9 %collective-permute-done.8 = bf16[4,176,128]{2,1,0:T(8,128)(2,1)S(1)} collective-permute-done((bf16[4,176,128]{2,1,0:T(8,128)(2,1)S(1)}, bf16[4,176,128]{2,1,0:T(8,128)(2,1)S(1)}, u32[]{:S(2)}, u32[]{:S(2)}) %collective-permute-start.8) | collective-permute-done | bytes 180256 | tf_op jit(solution)/shard_map/ppermute | solution.py:322
  95.0 14.2 %collective-permute-start.9 = (bf16[4,176,128]{2,1,0:T(8,128)(2,1)S(1)}, bf16[4,176,128]{2,1,0:T(8,128)(2,1)S(1)}, u32[]{:S(2)}, u32[]{:S(2)}) collective-permute-start(bf16[4,176,128]{2,1,0:T(8,128)(2,1)S(1)} %broadcast_select_fusion.4), channel_id=1, source_target_pairs={{0,32},{1,33},{2,34},{3,35},{4,36},{5,37},{6,38},{7,39},{8,40},{9,... | collective-permute-start | bytes 540680 | tf_op jit(solution)/shard_map/ppermute | solution.py:322
  109.3 0.1 add_bitcast_fusion.14
  109.4 34.5 %collective-permute-done.9 = bf16[4,176,128]{2,1,0:T(8,128)(2,1)S(1)} collective-permute-done((bf16[4,176,128]{2,1,0:T(8,128)(2,1)S(1)}, bf16[4,176,128]{2,1,0:T(8,128)(2,1)S(1)}, u32[]{:S(2)}, u32[]{:S(2)}) %collective-permute-start.9) | collective-permute-done | bytes 180256 | tf_op jit(solution)/shard_map/ppermute | solution.py:322
  143.9 0.7 broadcast_select_fusion.5.main_ref
  144.6 1.6 edges_of.1
  146.2 2.0 %collective-permute-start.10 = (bf16[4,56,128]{2,1,0:T(8,128)(2,1)}, bf16[4,56,128]{2,1,0:T(8,128)(2,1)S(1)}, u32[]{:S(2)}, u32[]{:S(2)}) collective-permute-start(bf16[4,56,128]{2,1,0:T(8,128)(2,1)} %get-tuple-element.8), channel_id=1, source_target_pairs={{0,64},{64,128},{128,192},{192,256},{256,320},{320,384},{384,448},... | collective-permute-start | bytes 172040 | tf_op jit(solution)/shard_map/ppermute | solution.py:17
  148.3 2.5 %collective-permute-start.11 = (bf16[4,56,128]{2,1,0:T(8,128)(2,1)}, bf16[4,56,128]{2,1,0:T(8,128)(2,1)S(1)}, u32[]{:S(2)}, u32[]{:S(2)}) collective-permute-start(bf16[4,56,128]{2,1,0:T(8,128)(2,1)} %get-tuple-element.9), channel_id=1, source_target_pairs={{0,960},{64,0},{128,64},{192,128},{256,192},{320,256},{384,320},{4... | collective-permute-start | bytes 172040 | tf_op jit(solution)/shard_map/ppermute | solution.py:17
  150.8 2.5 %multiply_add_fusion.disp_ref = f32[3,4,16,128]{3,2,1,0:T(8,128)} fusion(f32[3,4,20,132]{3,2,1,0:T(8,128)S(1)} %maximum_select_fusion, f32[4,16,128]{2,1,0:T(8,128)S(1)} %get-tuple-element.34, f32[4,16,128]{2,1,0:T(8,128)S(1)} %get-tuple-element.30, f32[4,16,128]{2,1,0:T(8,128)S(1)} %get-tuple-element.29, f32[4,16,128]{2,1,0:T(8,128)S(1)} %get-tuple-element.28, ...), kind=kLoop, calls=%fused_computation.107 | loop fusion | flops 6856704 | bytes 3342336 | tf_op jit(solution)/shard_map/add | solution.py:85
  153.3 0.0 collective-permute-done.10.below_ref
  153.3 0.0 copy-start.2
  153.3 2.8 %collective-permute-done.11.above_ref = bf16[4,56,128]{2,1,0:T(8,128)(2,1)S(1)} collective-permute-done((bf16[4,56,128]{2,1,0:T(8,128)(2,1)}, bf16[4,56,128]{2,1,0:T(8,128)(2,1)S(1)}, u32[]{:S(2)}, u32[]{:S(2)}) %collective-permute-start.11) | collective-permute-done | bytes 57376 | tf_op jit(solution)/shard_map/ppermute | solution.py:17
  156.1 0.0 copy-done.2
  156.1 0.6 copy-done.3
  156.7 13.6 %interpolate.1 = bf16[10,4,16,128]{3,2,1,0:T(8,128)(2,1)} custom-call(s32[1]{0:T(128)} %bitcast.place_ref, f32[3,4,16,128]{3,2,1,0:T(8,128)} %multiply_add_fusion.disp_ref, bf16[4,176,128]{2,1,0:T(8,128)(2,1)} %broadcast_select_fusion.5.main_ref, bf16[4,56,128]{2,1,0:T(8,128)(2,1)} %copy-done.2, bf16[4,56,128]{2,1,0:T(8,128)(2,1)} %copy-done.3), custom_call_target="tpu_custom_call" | custom-call | tf_op jit(solution)/shard_map/interpolate/pallas_call | solution.py:300
  (8 shorter events, 0.1 us)
Async XLA Ops:
  1.7 34.8 %collective-permute-start.1 = (f32[3,4,16,2]{3,2,1,0:T(8,128)S(1)}, f32[3,4,16,2]{3,2,1,0:T(8,128)S(1)}, u32[]{:S(2)}, u32[]{:S(2)}) collective-permute-start(f32[3,4,16,2]{3,2,1,0:T(8,128)S(1)} %get-tuple-element.73), channel_id=1, source_target_pairs={{0,63},{1,0},{2,1},{3,2},{4,3},{5,4},{6,5},{7,6},{8,7},{9,8},{10,9... | collective-permute-start | bytes 4616 | tf_op jit(solution)/shard_map/ppermute | solution.py:17
  22.6 13.9 %collective-permute-start = (f32[3,4,16,2]{3,2,1,0:T(8,128)S(1)}, f32[3,4,16,2]{3,2,1,0:T(8,128)S(1)}, u32[]{:S(2)}, u32[]{:S(2)}) collective-permute-start(f32[3,4,16,2]{3,2,1,0:T(8,128)S(1)} %get-tuple-element.72), channel_id=1, source_target_pairs={{0,1},{1,2},{2,3},{3,4},{4,5},{5,6},{6,7},{7,8},{8,9},{9,10},{10,1... | collective-permute-start | bytes 4616 | tf_op jit(solution)/shard_map/ppermute | solution.py:17
  24.5 0.7 copy-start.4
  28.2 16.1 %collective-permute-start.4 = (bf16[4,176,128]{2,1,0:T(8,128)(2,1)}, bf16[4,176,128]{2,1,0:T(8,128)(2,1)S(1)}, u32[]{:S(2)}, u32[]{:S(2)}) collective-permute-start(bf16[4,176,128]{2,1,0:T(8,128)(2,1)} %get-tuple-element.7), channel_id=1, source_target_pairs={{0,1},{1,2},{2,3},{3,4},{4,5},{5,6},{6,7},{7,8},{8,9},{9,10},{10,1... | collective-permute-start | bytes 540680 | tf_op jit(solution)/shard_map/ppermute | solution.py:322
  35.2 1.1 copy-start
  36.4 7.9 %copy-start.1 = (bf16[4,176,128]{2,1,0:T(8,128)(2,1)S(1)}, bf16[4,176,128]{2,1,0:T(8,128)(2,1)}, u32[]{:S(2)}) copy-start(bf16[4,176,128]{2,1,0:T(8,128)(2,1)} %get-tuple-element.7) | copy-start | bytes 540676
  36.6 9.7 %collective-permute-start.3 = (f32[3,4,2,132]{3,2,1,0:T(2,128)S(1)}, f32[3,4,2,132]{3,2,1,0:T(2,128)S(1)}, u32[]{:S(2)}, u32[]{:S(2)}) collective-permute-start(f32[3,4,2,132]{3,2,1,0:T(2,128)S(1)} %get-tuple-element.11), channel_id=1, source_target_pairs={{0,960},{64,0},{128,64},{192,128},{256,192},{320,256},{384,320},{4... | collective-permute-start | bytes 38024 | tf_op jit(solution)/shard_map/ppermute | solution.py:17
  38.5 7.8 %collective-permute-start.2 = (f32[3,4,2,132]{3,2,1,0:T(2,128)S(1)}, f32[3,4,2,132]{3,2,1,0:T(2,128)S(1)}, u32[]{:S(2)}, u32[]{:S(2)}) collective-permute-start(f32[3,4,2,132]{3,2,1,0:T(2,128)S(1)} %get-tuple-element.10), channel_id=1, source_target_pairs={{0,64},{64,128},{128,192},{192,256},{256,320},{320,384},{384,448},... | collective-permute-start | bytes 38024 | tf_op jit(solution)/shard_map/ppermute | solution.py:17
  44.4 6.2 %collective-permute-start.5 = (bf16[4,176,128]{2,1,0:T(8,128)(2,1)S(1)}, bf16[4,176,128]{2,1,0:T(8,128)(2,1)S(1)}, u32[]{:S(2)}, u32[]{:S(2)}) collective-permute-start(bf16[4,176,128]{2,1,0:T(8,128)(2,1)S(1)} %broadcast_select_fusion), channel_id=1, source_target_pairs={{0,2},{1,3},{2,4},{3,5},{4,6},{5,7},{6,8},{7,9},{8,10},{9,11},{10,... | collective-permute-start | bytes 540680 | tf_op jit(solution)/shard_map/ppermute | solution.py:322
  50.6 8.7 %collective-permute-start.6 = (bf16[4,176,128]{2,1,0:T(8,128)(2,1)S(1)}, bf16[4,176,128]{2,1,0:T(8,128)(2,1)S(1)}, u32[]{:S(2)}, u32[]{:S(2)}) collective-permute-start(bf16[4,176,128]{2,1,0:T(8,128)(2,1)S(1)} %broadcast_select_fusion.1), channel_id=1, source_target_pairs={{0,4},{1,5},{2,6},{3,7},{4,8},{5,9},{6,10},{7,11},{8,12},{9,13},{1... | collective-permute-start | bytes 540680 | tf_op jit(solution)/shard_map/ppermute | solution.py:322
  59.3 13.3 %collective-permute-start.7 = (bf16[4,176,128]{2,1,0:T(8,128)(2,1)S(1)}, bf16[4,176,128]{2,1,0:T(8,128)(2,1)S(1)}, u32[]{:S(2)}, u32[]{:S(2)}) collective-permute-start(bf16[4,176,128]{2,1,0:T(8,128)(2,1)S(1)} %broadcast_select_fusion.2), channel_id=1, source_target_pairs={{0,8},{1,9},{2,10},{3,11},{4,12},{5,13},{6,14},{7,15},{8,16},{9,17... | collective-permute-start | bytes 540680 | tf_op jit(solution)/shard_map/ppermute | solution.py:322
  72.7 22.3 %collective-permute-start.8 = (bf16[4,176,128]{2,1,0:T(8,128)(2,1)S(1)}, bf16[4,176,128]{2,1,0:T(8,128)(2,1)S(1)}, u32[]{:S(2)}, u32[]{:S(2)}) collective-permute-start(bf16[4,176,128]{2,1,0:T(8,128)(2,1)S(1)} %broadcast_select_fusion.3), channel_id=1, source_target_pairs={{0,16},{1,17},{2,18},{3,19},{4,20},{5,21},{6,22},{7,23},{8,24},{9,... | collective-permute-start | bytes 540680 | tf_op jit(solution)/shard_map/ppermute | solution.py:322
  95.0 48.9 %collective-permute-start.9 = (bf16[4,176,128]{2,1,0:T(8,128)(2,1)S(1)}, bf16[4,176,128]{2,1,0:T(8,128)(2,1)S(1)}, u32[]{:S(2)}, u32[]{:S(2)}) collective-permute-start(bf16[4,176,128]{2,1,0:T(8,128)(2,1)S(1)} %broadcast_select_fusion.4), channel_id=1, source_target_pairs={{0,32},{1,33},{2,34},{3,35},{4,36},{5,37},{6,38},{7,39},{8,40},{9,... | collective-permute-start | bytes 540680 | tf_op jit(solution)/shard_map/ppermute | solution.py:322
  146.2 7.1 %collective-permute-start.10 = (bf16[4,56,128]{2,1,0:T(8,128)(2,1)}, bf16[4,56,128]{2,1,0:T(8,128)(2,1)S(1)}, u32[]{:S(2)}, u32[]{:S(2)}) collective-permute-start(bf16[4,56,128]{2,1,0:T(8,128)(2,1)} %get-tuple-element.8), channel_id=1, source_target_pairs={{0,64},{64,128},{128,192},{192,256},{256,320},{320,384},{384,448},... | collective-permute-start | bytes 172040 | tf_op jit(solution)/shard_map/ppermute | solution.py:17
  148.3 7.8 %collective-permute-start.11 = (bf16[4,56,128]{2,1,0:T(8,128)(2,1)}, bf16[4,56,128]{2,1,0:T(8,128)(2,1)S(1)}, u32[]{:S(2)}, u32[]{:S(2)}) collective-permute-start(bf16[4,56,128]{2,1,0:T(8,128)(2,1)} %get-tuple-element.9), channel_id=1, source_target_pairs={{0,960},{64,0},{128,64},{192,128},{256,192},{320,256},{384,320},{4... | collective-permute-start | bytes 172040 | tf_op jit(solution)/shard_map/ppermute | solution.py:17
  153.3 2.8 %copy-start.2 = (bf16[4,56,128]{2,1,0:T(8,128)(2,1)}, bf16[4,56,128]{2,1,0:T(8,128)(2,1)S(1)}, u32[]{:S(2)}) copy-start(bf16[4,56,128]{2,1,0:T(8,128)(2,1)S(1)} %collective-permute-done.10.below_ref) | copy-start | bytes 172036
  156.1 0.6 copy-start.3
